TPU v7x, 32 devices: a whole 2x2x4 slice. The times are simulated.
32 devices in a mesh: sub: 2 (over y), row: 4 (over x, core), col: 4 (over z).
Axes of the slice: x: 2, y: 2, z: 4, core: 2. Of those that a mesh axis runs over, the one named last changes fastest.
Arguments:
- visibility: bfloat16 [2, 16, 512, 4096], P(None, 'sub', 'row', 'col'), may hold values from -13 to 13
- sky_model: bfloat16 [2, 16, 512, 4096], P(None, 'sub', 'row', 'col'), may hold values from -4 to 4, as said below
- antenna_flags: int32 [2, 512], P('sub'), may hold values 0 or 1
- gains_init: float32 [2, 16, 512], P(None, 'sub'), may hold values from -0.5 to 1.5
Outputs:
- gains: float32 [2, 16, 512], P(None, 'sub')
Inputs may be any that keep to these rules, and one draw needn't show every extreme that they name: `sky_model`: model visibility parts lie between -4 and 4.
All inputs are finite; a program needn't handle non-finite values.
Results may differ from a plain program's by a relative error of at most 0.0003.
Values sent between devices are 32-bit elements.
A program may use at most 64 MiB of HBM per device.

v0:
```python
import jax
import jax.numpy as jnp
from jax import lax
from jax.sharding import PartitionSpec as P

TIMES = 8
ITERS = 3


def subband_total(values):
    return lax.psum(values, "sub")


def update_gains(summed, previous):
    denominator = summed[:, 2, :] + 1.0
    quotient = jnp.stack([summed[:, 0, :] / denominator, summed[:, 1, :] / denominator], axis=0)
    updated = 0.5 * (quotient + previous)
    chan_mean = jnp.sum(updated, axis=1) / updated.shape[1]
    overall = subband_total(chan_mean) / lax.axis_size("sub")
    return updated + 0.5 * (overall - chan_mean)[:, None, :]


def time_total(values, selector):
    return jnp.einsum(
        "crk,kq->crq",
        values,
        selector,
        precision=lax.Precision.HIGHEST,
        preferred_element_type=jnp.float32,
    )


def contract(matrix, vector):
    return jnp.einsum("cpq,cq->cp", matrix, vector, precision=lax.Precision.HIGHEST)


def body(visibility, sky_model, antenna_flags, gains_init):
    block_rows = visibility.shape[2]
    wide_cols = visibility.shape[3]
    block_cols = wide_cols // TIMES
    row_at = lax.axis_index("row") * block_rows
    col_at = lax.axis_index("col") * block_cols
    flag_value = antenna_flags[0].astype(jnp.float32)
    row_flag = lax.dynamic_slice_in_dim(flag_value, row_at, block_rows)
    col_flag = lax.dynamic_slice_in_dim(flag_value, col_at, block_cols)
    row_ids = row_at + lax.iota(jnp.int32, block_rows)
    col_ids = col_at + lax.iota(jnp.int32, block_cols)
    weight = (
        row_flag[:, None]
        * col_flag[None, :]
        * (row_ids[:, None] != col_ids[None, :]).astype(jnp.float32)
    )
    selector = (
        lax.iota(jnp.int32, wide_cols)[:, None] // TIMES == lax.iota(jnp.int32, block_cols)[None, :]
    ).astype(jnp.float32)
    vis_re = visibility[0].astype(jnp.float32)
    vis_im = visibility[1].astype(jnp.float32)
    mod_re = sky_model[0].astype(jnp.float32)
    mod_im = sky_model[1].astype(jnp.float32)
    cross_re = time_total(vis_re * mod_re + vis_im * mod_im, selector) * weight
    cross_im = time_total(vis_im * mod_re - vis_re * mod_im, selector) * weight
    power_sum = time_total(mod_re * mod_re + mod_im * mod_im, selector) * weight
    gain_values = gains_init
    for step_index in range(ITERS):
        col_gains = lax.dynamic_slice_in_dim(gain_values, col_at, block_cols, 2)
        gain_re = col_gains[0]
        gain_im = col_gains[1]
        num_re = contract(cross_re, gain_re) - contract(cross_im, gain_im)
        num_im = contract(cross_re, gain_im) + contract(cross_im, gain_re)
        denominator = contract(power_sum, gain_re * gain_re + gain_im * gain_im)
        partial_value = jnp.stack([num_re, num_im, denominator], axis=1)
        summed = lax.psum(partial_value, "col")
        previous = lax.dynamic_slice_in_dim(gain_values, row_at, block_rows, 2)
        gain_block = update_gains(summed, previous)
        gain_values = lax.all_gather(gain_block, "row", axis=2, tiled=True)
    return gain_values


def solution(mesh):
    return jax.shard_map(
        body,
        mesh=mesh,
        in_specs=(
            P(None, "sub", "row", "col"),
            P(None, "sub", "row", "col"),
            P("sub", None),
            P(None, "sub", None),
        ),
        out_specs=P(None, "sub", None),
        check_vma=False,
    )
```

profile of v0, /device:TPU:0, one launch (start us, length us, event | category | flops | bytes accessed | tf_op | source)
XLA Modules:
  0.0 111.2 jit_solution(4182115625880762958)
XLA Ops:
  1.5 6.6 %fusion.25 = f32[8,128,128]{2,1,0:T(8,128)S(1)} fusion(bf16[2,8,128,1024]{3,2,1,0:T(8,128)(2,1)} %param.4, bf16[2,8,128,1024]{3,2,1,0:T(8,128)(2,1)} %param.5, f32[128,128]{1,0:T(8,128)S(1)} %multiply_select_fusion, s32[1024]{0:T(1024)S(1)} %add_select_fusion), kind=kOutput, calls=%fused_computation.26 | convolution fusion | flops 1618214912 | bytes 8982528 | tf_op jit(solution)/shard_map/crk,kq->crq/dot_general | solution.py:24
  8.1 0.9 fusion.61
  9.0 0.9 fusion.59
  10.0 3.0 %fusion.28 = f32[8,128,128]{2,1,0:T(8,128)S(1)} fusion(bf16[2,8,128,1024]{3,2,1,0:T(8,128)(2,1)S(1)} %copy-done.1, bf16[2,8,128,1024]{3,2,1,0:T(8,128)(2,1)S(1)} %copy-done.2, f32[128,128]{1,0:T(8,128)S(1)} %multiply_select_fusion, s32[1024]{0:T(1024)S(1)} %add_select_fusion), kind=kOutput, calls=%fused_computation.27 | convolution fusion | flops 1618214912 | bytes 8982528 | tf_op jit(solution)/shard_map/crk,kq->crq/dot_general | solution.py:24
  13.9 0.9 fusion.58
  14.8 2.7 %fusion.22 = f32[8,128,128]{2,1,0:T(8,128)S(1)} fusion(bf16[2,8,128,1024]{3,2,1,0:T(8,128)(2,1)S(1)} %copy-done.2, f32[128,128]{1,0:T(8,128)S(1)} %multiply_select_fusion, s32[1024]{0:T(1024)S(1)} %add_select_fusion), kind=kOutput, calls=%fused_computation.25 | convolution fusion | flops 1616117760 | bytes 4788224 | tf_op jit(solution)/shard_map/crk,kq->crq/dot_general | solution.py:24
  17.5 0.9 fusion.62
  18.4 20.4 %psum.42 = f32[8,3,128]{2,0,1:T(8,128)S(1)} all-reduce(f32[8,3,128]{2,0,1:T(8,128)S(1)} %pad_maximum_fusion), channel_id=1, replica_groups=mesh['sub'=2,'row'=4,'col'=4] {'col'}, use_global_device_ids=true, to_apply=%region_0.1 | all-reduce | flops 3072 | bytes 24576 | tf_op jit(solution)/shard_map/psum | solution.py:72
  38.9 4.9 %psum.43 = f32[2,128]{1,0:T(2,128)S(1)} all-reduce(f32[2,128]{1,0:T(2,128)S(1)} %broadcast_multiply_fusion.2), channel_id=1, replica_groups=mesh['sub'=2,'row'=4,'col'=4] {'sub'}, use_global_device_ids=true, to_apply=%region_2.3 | all-reduce | flops 256 | bytes 2048 | tf_op jit(solution)/shard_map/psum | solution.py:11
  43.9 5.2 %all_gather.9 = f32[2,8,512]{2,1,0:T(8,128)S(1)} all-gather(f32[2,8,128]{2,1,0:T(8,128)S(1)} %broadcast_add_fusion.2), channel_id=1, replica_groups=mesh['sub'=2,'row'=4,'col'=4] {'row'}, dimensions={2}, use_global_device_ids=true | all-gather | bytes 40960 | tf_op jit(solution)/shard_map/all_gather | solution.py:75
  50.0 0.9 fusion.66
  50.9 0.9 fusion.63
  51.8 0.9 fusion.65
  52.8 0.9 fusion.64
  53.7 15.5 %psum.44 = f32[8,3,128]{2,0,1:T(8,128)S(1)} all-reduce(f32[8,3,128]{2,0,1:T(8,128)S(1)} %pad_maximum_fusion.1), channel_id=1, replica_groups=mesh['sub'=2,'row'=4,'col'=4] {'col'}, use_global_device_ids=true, to_apply=%region_3.4 | all-reduce | flops 3072 | bytes 24576 | tf_op jit(solution)/shard_map/psum | solution.py:72
  69.3 4.9 %psum.45 = f32[2,128]{1,0:T(2,128)S(1)} all-reduce(f32[2,128]{1,0:T(2,128)S(1)} %broadcast_multiply_fusion.1), channel_id=1, replica_groups=mesh['sub'=2,'row'=4,'col'=4] {'sub'}, use_global_device_ids=true, to_apply=%region_5.6 | all-reduce | flops 256 | bytes 2048 | tf_op jit(solution)/shard_map/psum | solution.py:11
  74.3 5.2 %all_gather.10 = f32[2,8,512]{2,1,0:T(8,128)S(1)} all-gather(f32[2,8,128]{2,1,0:T(8,128)S(1)} %broadcast_add_fusion.1), channel_id=1, replica_groups=mesh['sub'=2,'row'=4,'col'=4] {'row'}, dimensions={2}, use_global_device_ids=true | all-gather | bytes 40960 | tf_op jit(solution)/shard_map/all_gather | solution.py:75
  80.4 0.9 fusion.71
  81.3 0.9 fusion.69
  82.2 0.9 fusion.70
  83.2 0.9 fusion.68
  84.1 16.2 %psum.46 = f32[8,3,128]{2,0,1:T(8,128)S(1)} all-reduce(f32[8,3,128]{2,0,1:T(8,128)S(1)} %pad_maximum_fusion.2), channel_id=1, replica_groups=mesh['sub'=2,'row'=4,'col'=4] {'col'}, use_global_device_ids=true, to_apply=%region_6.7 | all-reduce | flops 3072 | bytes 24576 | tf_op jit(solution)/shard_map/psum | solution.py:72
  100.4 4.9 %psum.47 = f32[2,128]{1,0:T(2,128)S(1)} all-reduce(f32[2,128]{1,0:T(2,128)S(1)} %broadcast_multiply_fusion), channel_id=1, replica_groups=mesh['sub'=2,'row'=4,'col'=4] {'sub'}, use_global_device_ids=true, to_apply=%region_8.9 | all-reduce | flops 256 | bytes 2048 | tf_op jit(solution)/shard_map/psum | solution.py:11
  105.3 5.2 %all_gather.11 = f32[2,8,512]{2,1,0:T(8,128)S(1)} all-gather(f32[2,8,128]{2,1,0:T(8,128)S(1)} %broadcast_add_fusion), channel_id=1, replica_groups=mesh['sub'=2,'row'=4,'col'=4] {'row'}, dimensions={2}, use_global_device_ids=true | all-gather | bytes 40960 | tf_op jit(solution)/shard_map/all_gather | solution.py:75
  (42 shorter events, 5.1 us)
Async XLA Ops:
  1.5 8.4 %copy-start.1 = (bf16[2,8,128,1024]{3,2,1,0:T(8,128)(2,1)S(1)}, bf16[2,8,128,1024]{3,2,1,0:T(8,128)(2,1)}, u32[]{:S(2)}) copy-start(bf16[2,8,128,1024]{3,2,1,0:T(8,128)(2,1)} %param.4) | copy-start | bytes 12582916
  1.5 8.4 %copy-start.2 = (bf16[2,8,128,1024]{3,2,1,0:T(8,128)(2,1)S(1)}, bf16[2,8,128,1024]{3,2,1,0:T(8,128)(2,1)}, u32[]{:S(2)}) copy-start(bf16[2,8,128,1024]{3,2,1,0:T(8,128)(2,1)} %param.5) | copy-start | bytes 12582916
  13.9 25.0 %copy-start = (f32[2,8,512]{2,1,0:T(8,128)S(1)}, f32[2,8,512]{2,1,0:T(8,128)}, u32[]{:S(2)}) copy-start(f32[2,8,512]{2,1,0:T(8,128)} %param.7) | copy-start | bytes 98308
where the time goes:
time: 112 us; the launch traced here: 111 us
  blocking collectives  82.5 us (74%)
  matrix products  26.1 us (23%)
  other arithmetic  1.73 us (2%)
    psum x3, blocking collectives, body(): summed = lax.psum(partial_value, 'col')  52.2 us
    all_gather x3, blocking collectives, body(): gain_values = lax.all_gather(gain_block, 'row', axis=2, tiled=True)  15.6 us
    psum x3, blocking collectives, subband_total(): return lax.psum(values, 'sub')  14.8 us
    dot_general x15, matrix products, contract(): jnp.einsum('cpq,cq->cp', matrix, vector, precision=lax.Precision.HIGHEST)  13.9 us
    dot_general x3, matrix products, time_total(): jnp.einsum('crk,kq->crq', values, selector, precision=lax.Precision.HIGHE...  12.3 us

commit v1 on v0

--- a/solution.py
+++ b/solution.py
@@ -5,6 +5,11 @@
 
 TIMES = 8
 ITERS = 3
+
+
+def _divide_waves(load, axis_id):
+    v_next = lax.all_gather(load, axis_id).sum(axis=0)
+    return v_next
 
 
 def subband_total(values):
@@ -69,7 +74,7 @@
         num_im = contract(cross_re, gain_im) + contract(cross_im, gain_re)
         denominator = contract(power_sum, gain_re * gain_re + gain_im * gain_im)
         partial_value = jnp.stack([num_re, num_im, denominator], axis=1)
-        summed = lax.psum(partial_value, "col")
+        summed = _divide_waves(partial_value, "col")
         previous = lax.dynamic_slice_in_dim(gain_values, row_at, block_rows, 2)
         gain_block = update_gains(summed, previous)
         gain_values = lax.all_gather(gain_block, "row", axis=2, tiled=True)

time: 112 us -> 100 us (0.89)
  blocking collectives: 82.5 us -> 71.5 us
    psum x3 -> x0, blocking collectives: 52.2 us -> none  [body(): summed = lax.psum(partial_value, 'col')]
    all_gather x0 -> x3, blocking collectives: none -> 40.9 us  [_divide_waves(): v_next = lax.all_gather(load, axis_id).sum(axis=0)]
where the time goes in v1:
time: 100 us
  blocking collectives  71.5 us (72%)
  matrix products  26.1 us (26%)
  other arithmetic  1.76 us (2%)
    all_gather x3, blocking collectives, _divide_waves(): v_next = lax.all_gather(load, axis_id).sum(axis=0)  40.9 us
    all_gather x3, blocking collectives, body(): gain_values = lax.all_gather(gain_block, 'row', axis=2, tiled=True)  15.6 us
    psum x3, blocking collectives, subband_total(): return lax.psum(values, 'sub')  15 us
    dot_general x15, matrix products, contract(): jnp.einsum('cpq,cq->cp', matrix, vector, precision=lax.Precision.HIGHEST)  13.9 us
    dot_general x3, matrix products, time_total(): jnp.einsum('crk,kq->crq', values, selector, precision=lax.Precision.HIGHE...  12.3 us

profile of v1, /device:TPU:0, one launch (start us, length us, event | category | flops | bytes accessed | tf_op | source)
XLA Modules:
  0.0 100.1 jit_solution(1204330458822717510)
XLA Ops:
  1.5 6.6 %fusion.25 = f32[8,128,128]{2,1,0:T(8,128)S(1)} fusion(bf16[2,8,128,1024]{3,2,1,0:T(8,128)(2,1)} %param.4, bf16[2,8,128,1024]{3,2,1,0:T(8,128)(2,1)} %param.5, f32[128,128]{1,0:T(8,128)S(1)} %multiply_select_fusion, s32[1024]{0:T(1024)S(1)} %add_select_fusion), kind=kOutput, calls=%fused_computation.26 | convolution fusion | flops 1618214912 | bytes 8982528 | tf_op jit(solution)/shard_map/crk,kq->crq/dot_general | solution.py:29
  8.1 0.9 fusion.61
  9.0 0.9 fusion.59
  10.0 3.0 %fusion.28 = f32[8,128,128]{2,1,0:T(8,128)S(1)} fusion(bf16[2,8,128,1024]{3,2,1,0:T(8,128)(2,1)S(1)} %copy-done.1, bf16[2,8,128,1024]{3,2,1,0:T(8,128)(2,1)S(1)} %copy-done.2, f32[128,128]{1,0:T(8,128)S(1)} %multiply_select_fusion, s32[1024]{0:T(1024)S(1)} %add_select_fusion), kind=kOutput, calls=%fused_computation.27 | convolution fusion | flops 1618214912 | bytes 8982528 | tf_op jit(solution)/shard_map/crk,kq->crq/dot_general | solution.py:29
  13.9 0.9 fusion.58
  14.8 2.7 %fusion.22 = f32[8,128,128]{2,1,0:T(8,128)S(1)} fusion(bf16[2,8,128,1024]{3,2,1,0:T(8,128)(2,1)S(1)} %copy-done.2, f32[128,128]{1,0:T(8,128)S(1)} %multiply_select_fusion, s32[1024]{0:T(1024)S(1)} %add_select_fusion), kind=kOutput, calls=%fused_computation.25 | convolution fusion | flops 1616117760 | bytes 4788224 | tf_op jit(solution)/shard_map/crk,kq->crq/dot_general | solution.py:29
  17.5 0.9 fusion.62
  18.4 14.8 %all-gather = f32[32,3,128]{2,0,1:T(8,128)S(1)} all-gather(f32[8,3,128]{2,0,1:T(8,128)S(1)} %pad_maximum_fusion), channel_id=2, replica_groups=mesh['sub'=2,'row'=4,'col'=4] {'col'}, dimensions={0}, use_global_device_ids=true | all-gather | bytes 61440 | tf_op jit(solution)/shard_map/all_gather | solution.py:11
  33.3 5.1 %psum.21 = f32[2,128]{1,0:T(2,128)S(1)} all-reduce(f32[2,128]{1,0:T(2,128)S(1)} %broadcast_multiply_fusion.2), channel_id=1, replica_groups=mesh['sub'=2,'row'=4,'col'=4] {'sub'}, use_global_device_ids=true, to_apply=%region_2.3 | all-reduce | flops 256 | bytes 2048 | tf_op jit(solution)/shard_map/psum | solution.py:16
  38.4 5.2 %all_gather.29 = f32[2,8,512]{2,1,0:T(8,128)S(1)} all-gather(f32[2,8,128]{2,1,0:T(8,128)S(1)} %broadcast_add_fusion.2), channel_id=1, replica_groups=mesh['sub'=2,'row'=4,'col'=4] {'row'}, dimensions={2}, use_global_device_ids=true | all-gather | bytes 40960 | tf_op jit(solution)/shard_map/all_gather | solution.py:80
  44.5 0.9 fusion.66
  45.4 0.9 fusion.63
  46.4 0.9 fusion.65
  47.3 0.9 fusion.64
  48.3 13.1 %all-gather.1 = f32[32,3,128]{2,0,1:T(8,128)S(1)} all-gather(f32[8,3,128]{2,0,1:T(8,128)S(1)} %pad_maximum_fusion.1), channel_id=3, replica_groups=mesh['sub'=2,'row'=4,'col'=4] {'col'}, dimensions={0}, use_global_device_ids=true | all-gather | bytes 61440 | tf_op jit(solution)/shard_map/all_gather | solution.py:11
  61.4 4.9 %psum.22 = f32[2,128]{1,0:T(2,128)S(1)} all-reduce(f32[2,128]{1,0:T(2,128)S(1)} %broadcast_multiply_fusion.1), channel_id=1, replica_groups=mesh['sub'=2,'row'=4,'col'=4] {'sub'}, use_global_device_ids=true, to_apply=%region_5.6 | all-reduce | flops 256 | bytes 2048 | tf_op jit(solution)/shard_map/psum | solution.py:16
  66.4 5.2 %all_gather.32 = f32[2,8,512]{2,1,0:T(8,128)S(1)} all-gather(f32[2,8,128]{2,1,0:T(8,128)S(1)} %broadcast_add_fusion.1), channel_id=1, replica_groups=mesh['sub'=2,'row'=4,'col'=4] {'row'}, dimensions={2}, use_global_device_ids=true | all-gather | bytes 40960 | tf_op jit(solution)/shard_map/all_gather | solution.py:80
  72.5 0.9 fusion.71
  73.4 0.9 fusion.69
  74.3 0.9 fusion.70
  75.3 0.9 fusion.68
  76.2 13.1 %all-gather.2 = f32[32,3,128]{2,0,1:T(8,128)S(1)} all-gather(f32[8,3,128]{2,0,1:T(8,128)S(1)} %pad_maximum_fusion.2), channel_id=4, replica_groups=mesh['sub'=2,'row'=4,'col'=4] {'col'}, dimensions={0}, use_global_device_ids=true | all-gather | bytes 61440 | tf_op jit(solution)/shard_map/all_gather | solution.py:11
  89.3 4.9 %psum.23 = f32[2,128]{1,0:T(2,128)S(1)} all-reduce(f32[2,128]{1,0:T(2,128)S(1)} %broadcast_multiply_fusion), channel_id=1, replica_groups=mesh['sub'=2,'row'=4,'col'=4] {'sub'}, use_global_device_ids=true, to_apply=%region_8.9 | all-reduce | flops 256 | bytes 2048 | tf_op jit(solution)/shard_map/psum | solution.py:16
  94.3 5.2 %all_gather.35 = f32[2,8,512]{2,1,0:T(8,128)S(1)} all-gather(f32[2,8,128]{2,1,0:T(8,128)S(1)} %broadcast_add_fusion), channel_id=1, replica_groups=mesh['sub'=2,'row'=4,'col'=4] {'row'}, dimensions={2}, use_global_device_ids=true | all-gather | bytes 40960 | tf_op jit(solution)/shard_map/all_gather | solution.py:80
  (45 shorter events, 5.1 us)
Async XLA Ops:
  1.5 8.4 %copy-start.1 = (bf16[2,8,128,1024]{3,2,1,0:T(8,128)(2,1)S(1)}, bf16[2,8,128,1024]{3,2,1,0:T(8,128)(2,1)}, u32[]{:S(2)}) copy-start(bf16[2,8,128,1024]{3,2,1,0:T(8,128)(2,1)} %param.4) | copy-start | bytes 12582916
  1.5 8.4 %copy-start.2 = (bf16[2,8,128,1024]{3,2,1,0:T(8,128)(2,1)S(1)}, bf16[2,8,128,1024]{3,2,1,0:T(8,128)(2,1)}, u32[]{:S(2)}) copy-start(bf16[2,8,128,1024]{3,2,1,0:T(8,128)(2,1)} %param.5) | copy-start | bytes 12582916
  13.9 19.4 %copy-start = (f32[2,8,512]{2,1,0:T(8,128)S(1)}, f32[2,8,512]{2,1,0:T(8,128)}, u32[]{:S(2)}) copy-start(f32[2,8,512]{2,1,0:T(8,128)} %param.7) | copy-start | bytes 98308
